TPU v7x, 32 devices: a whole 2x2x4 slice. The times are simulated.
32 devices in a mesh: row: 4 (over z), col: 8 (over y, x, core).
Axes of the slice: x: 2, y: 2, z: 4, core: 2. Of those that a mesh axis runs over, the one named last changes fastest.
Arguments:
- grad: float32 [8192, 14336], P(('row', 'col')), may hold values from -30 to 30
- momentum: float32 [8192, 14336], P(('row', 'col')), may hold values from -6 to 6
- weight: float32 [8192, 14336], P(('row', 'col')), may hold values from -0.75 to 0.75
Outputs:
- new_weight: float32 [8192, 14336], P('row', 'col')
- new_momentum: float32 [8192, 14336], P('row', 'col')
All inputs are finite; a program needn't handle non-finite values.
Results may differ from a plain program's by a relative error of at most 0.00002.
Values sent between devices are 32-bit elements; how exact they have to be, the bound alone decides.
No kernel may reach another device: no remote copies, remote signals or barrier semaphores. Data moves between devices by JAX's collectives and lax.ppermute only.
A program may use at most 192 MiB of HBM per device.

v0:
```python
import math

import jax
import jax.numpy as jnp
from jax import lax
from jax.sharding import PartitionSpec as P

D = 8192
FF = 14336


def update_state(total, grad, momentum, weight):
    limit = jnp.float32(math.sqrt(D * FF))
    factor = jnp.minimum(jnp.float32(1.0), limit / (jnp.sqrt(total) + jnp.float32(1e-06)))
    new_momentum = jnp.float32(0.9) * momentum + factor * grad
    new_weight = weight - jnp.float32(0.1) * new_momentum
    return (new_weight, new_momentum)


def body(grad, momentum, weight):
    total = lax.psum(jnp.sum(grad * grad), ("row", "col"))
    local_weight, local_momentum = update_state(total, grad, momentum, weight)
    new_weight, new_momentum = (
        lax.all_to_all(local_weight, "col", split_axis=1, concat_axis=0, tiled=True),
        lax.all_to_all(local_momentum, "col", split_axis=1, concat_axis=0, tiled=True),
    )
    return (new_weight, new_momentum)


def solution(mesh):
    in_specs = (P(("row", "col"), None), P(("row", "col"), None), P(("row", "col"), None))
    out_specs = (P("row", "col"), P("row", "col"))
    return jax.shard_map(body, mesh=mesh, in_specs=in_specs, out_specs=out_specs, check_vma=False)
```

profile of v0, /device:TPU:0, one launch (start us, length us, event | category | flops | bytes accessed | tf_op | source)
XLA Modules:
  0.0 447.5 jit_solution(14981939035309159026)
XLA Ops:
  0.6 9.6 %multiply_reduce_fusion = f32[]{:T(128)} fusion(f32[256,14336]{1,0:T(8,128)} %param.3), kind=kLoop, calls=%fused_computation.4 | loop fusion | flops 7340031 | bytes 14680068 | tf_op jit(solution)/shard_map/reduce_sum | solution.py:21
  10.2 42.2 %psum.7 = f32[]{:T(128)} all-reduce(f32[]{:T(128)} %multiply_reduce_fusion), channel_id=1, replica_groups=mesh['row'=4,'col'=8] {'row','col'}, use_global_device_ids=true, to_apply=%region_1.0 | all-reduce | flops 1 | bytes 8 | tf_op jit(solution)/shard_map/psum | solution.py:21
  53.1 25.5 %multiply_subtract_fusion = (f32[256,14336]{1,0:T(8,128)}, f32[256,14336]{1,0:T(8,128)}) fusion(f32[256,14336]{1,0:T(8,128)} %param.5, f32[256,14336]{1,0:T(8,128)} %param.3, f32[]{:T(128)S(6)} %min_shard_map.3, f32[256,14336]{1,0:T(8,128)} %param.4), kind=kLoop, calls=%fused_computation.2 | loop fusion | flops 18350080 | bytes 73400320 | tf_op jit(solution)/shard_map/sub | solution.py:16
  78.6 11.8 %copy.11 = f32[32,8,8,1792]{3,2,0,1:T(8,128)} copy(f32[32,8,8,1792]{3,2,1,0:T(8,128)} %bitcast.17) | data formatting | bytes 29360128 | tf_op jit(solution)/shard_map/all_to_all | solution.py:25
  90.3 5.5 %all-to-all-start.1 = ((f32[256,8,1792]{2,0,1:T(8,128)}), f32[256,8,1792]{2,0,1:T(8,128)}, u32[]{:S(2)}, u32[]{:S(2)}) async-start(f32[256,8,1792]{2,0,1:T(8,128)} %bitcast.15), calls=%async_computation.1 | async-start | bytes 29360128 | tf_op jit(solution)/shard_map/all_to_all | solution.py:25
  95.9 12.0 %copy.12 = f32[32,8,8,1792]{3,2,0,1:T(8,128)} copy(f32[32,8,8,1792]{3,2,1,0:T(8,128)} %bitcast.16) | data formatting | bytes 29360128 | tf_op jit(solution)/shard_map/all_to_all | solution.py:24
  107.9 149.4 %all-to-all-done.1 = f32[256,8,1792]{2,0,1:T(8,128)} async-done(((f32[256,8,1792]{2,0,1:T(8,128)}), f32[256,8,1792]{2,0,1:T(8,128)}, u32[]{:S(2)}, u32[]{:S(2)}) %all-to-all-start.1) | async-done | bytes 14680096 | tf_op jit(solution)/shard_map/all_to_all | solution.py:25
  257.3 5.5 %all-to-all-start = ((f32[256,8,1792]{2,0,1:T(8,128)}), f32[256,8,1792]{2,0,1:T(8,128)}, u32[]{:S(2)}, u32[]{:S(2)}) async-start(f32[256,8,1792]{2,0,1:T(8,128)} %bitcast.14), calls=%async_computation | async-start | bytes 29360128 | tf_op jit(solution)/shard_map/all_to_all | solution.py:24
  262.9 161.5 %all-to-all-done = f32[256,8,1792]{2,0,1:T(8,128)} async-done(((f32[256,8,1792]{2,0,1:T(8,128)}), f32[256,8,1792]{2,0,1:T(8,128)}, u32[]{:S(2)}, u32[]{:S(2)}) %all-to-all-start) | async-done | bytes 14680096 | tf_op jit(solution)/shard_map/all_to_all | solution.py:24
  424.3 11.6 %copy.15 = f32[2048,1792]{1,0:T(8,128)} copy(f32[2048,1792]{1,0:T(8,128)} %bitcast.1) | data formatting | bytes 29360128
  435.9 11.6 %copy.16 = f32[2048,1792]{1,0:T(8,128)} copy(f32[2048,1792]{1,0:T(8,128)} %bitcast.3) | data formatting | bytes 29360128
Async XLA Ops:
  90.3 167.0 %all-to-all-start.1 = ((f32[256,8,1792]{2,0,1:T(8,128)}), f32[256,8,1792]{2,0,1:T(8,128)}, u32[]{:S(2)}, u32[]{:S(2)}) async-start(f32[256,8,1792]{2,0,1:T(8,128)} %bitcast.15), calls=%async_computation.1 | async-start | bytes 29360128 | tf_op jit(solution)/shard_map/all_to_all | solution.py:25
  257.3 167.0 %all-to-all-start = ((f32[256,8,1792]{2,0,1:T(8,128)}), f32[256,8,1792]{2,0,1:T(8,128)}, u32[]{:S(2)}, u32[]{:S(2)}) async-start(f32[256,8,1792]{2,0,1:T(8,128)} %bitcast.14), calls=%async_computation | async-start | bytes 29360128 | tf_op jit(solution)/shard_map/all_to_all | solution.py:24
where the time goes:
time: 448 us; the launch traced here: 447 us
  waiting for transfers between devices  311 us (69%)
  local copies, waits for them, and re-layouts  47 us (10%)
  blocking collectives  42.2 us (9%)
  other arithmetic  35 us (8%)
  starting transfers between devices  11.1 us (2%)
    all_to_all x1, waiting for transfers between devices, body(): lax.all_to_all(local_weight, 'col', split_axis=1, concat_axis=0, tiled=True)  161 us
    all_to_all x1, waiting for transfers between devices, body(): lax.all_to_all(local_momentum, 'col', split_axis=1, concat_axis=0, tiled=...  149 us
    psum x1, blocking collectives, body(): total = lax.psum(jnp.sum(grad * grad), ('row', 'col'))  42.2 us
    sub x1, other arithmetic, update_state(): new_weight = weight - jnp.float32(0.1) * new_momentum  25.5 us
    unnamed x2, local copies, waits for them, and re-layouts  23.2 us
    all_to_all x1, local copies, waits for them, and re-layouts, body(): lax.all_to_all(local_weight, 'col', split_axis=1, concat_axis=0, tiled=True)  12 us
    all_to_all x1, local copies, waits for them, and re-layouts, body(): lax.all_to_all(local_momentum, 'col', split_axis=1, concat_axis=0, tiled=...  11.8 us
    reduce_sum x1, other arithmetic, body(): total = lax.psum(jnp.sum(grad * grad), ('row', 'col'))  9.55 us
  transfers between devices with their start and end apart: 2, of which 2 were waited for; matrix products, arithmetic and copies ran while one was open for 3% of the time, Pallas kernels for 0%

commit v1 on v0

v1 whole, which is shorter than its diff:
```python
import math

import jax
import jax.numpy as jnp
from jax import lax
from jax.experimental import pallas as pl
from jax.experimental.pallas import tpu as pltpu
from jax.sharding import PartitionSpec as P


F32 = jnp.float32
LANES = 128


def hop(x, axis, k, n):
    return lax.ppermute(x, axis, [(i, i ^ k) for i in range(n)])


def cost(passes, rows, cols):
    return pl.CostEstimate(flops=4 * rows * cols, bytes_accessed=4 * passes * rows * cols, transcendentals=0)


PARAMS = pltpu.CompilerParams(vmem_limit_bytes=67043328)


def block_rows(rows, start, most=64):
    b = most
    while rows % b or start % b:
        b //= 2
    return b


def copy_kernel(at, x_ref, o_ref):
    o_ref[...] = x_ref[...]


def cut(x, at, cols, start, rows):
    b = block_rows(rows, start)
    s = start // b
    return pl.pallas_call(
        copy_kernel,
        grid_spec=pltpu.PrefetchScalarGridSpec(
            num_scalar_prefetch=1, grid=(rows // b,),
            in_specs=[pl.BlockSpec((b, cols), lambda i, at: (s + i, at[0]))],
            out_specs=pl.BlockSpec((b, cols), lambda i, at: (i, 0))),
        out_shape=jax.ShapeDtypeStruct((rows, cols), F32),
        cost_estimate=cost(2, rows, cols), name="cut", compiler_params=PARAMS,
    )(at, x)


def calc_kernel(at, factor, m_ref, g_ref, o_ref):
    o_ref[...] = F32(0.9) * m_ref[...] + factor[0] * g_ref[...]


def calc(m, g, factor, at, cols, start, rows):
    b = block_rows(rows, start)
    s = start // b
    spec = pl.BlockSpec((b, cols), lambda i, at: (s + i, at[0]))
    return pl.pallas_call(
        calc_kernel,
        grid_spec=pltpu.PrefetchScalarGridSpec(
            num_scalar_prefetch=1, grid=(rows // b,),
            in_specs=[pl.BlockSpec(memory_space=pltpu.SMEM), spec, spec],
            out_specs=pl.BlockSpec((b, cols), lambda i, at: (i, 0))),
        out_shape=jax.ShapeDtypeStruct((rows, cols), F32),
        cost_estimate=cost(3, rows, cols), name="calc", compiler_params=PARAMS,
    )(at, factor, m, g)


def finish_kernel(at, w_ref, m_ref, *refs):
    nw_ref, nm_ref = refs[-2:]
    m = m_ref[...]
    nm_ref[...] = m
    nw_ref[...] = w_ref[...] - F32(0.1) * m


def finish(at, w, m, outs, shape, piece, start):
    rows, cols = w.shape
    b = block_rows(rows, start)
    s, p = start // b, piece // b
    spec = pl.BlockSpec((b, cols), lambda i, at: (i, 0))
    ospec = pl.BlockSpec((b, cols), lambda i, at: (at[0] * p + s + i, 0))
    hbm = pl.BlockSpec(memory_space=pl.ANY)
    outs = outs or ()
    return pl.pallas_call(
        finish_kernel,
        grid_spec=pltpu.PrefetchScalarGridSpec(
            num_scalar_prefetch=1, grid=(rows // b,),
            in_specs=[spec, spec] + [hbm] * len(outs), out_specs=[ospec, ospec]),
        out_shape=[jax.ShapeDtypeStruct(shape, F32)] * 2,
        input_output_aliases={3: 0, 4: 1} if outs else {},
        cost_estimate=cost(4, rows, cols), name="finish", compiler_params=PARAMS,
    )(at, w, m, *outs)


def own_kernel(at, factor, w_ref, m_ref, g_ref, nw_ref, nm_ref):
    m = F32(0.9) * m_ref[...] + factor[0] * g_ref[...]
    nm_ref[...] = m
    nw_ref[...] = w_ref[...] - F32(0.1) * m


def own(at, factor, w, m, g, n):
    rows, cols = w.shape[0], w.shape[1] // n
    b = block_rows(rows, 0)
    t = rows // b
    spec = pl.BlockSpec((b, cols), lambda i, at: (i, at[0]))
    ospec = pl.BlockSpec((b, cols), lambda i, at: (at[0] * t + i, 0))
    return pl.pallas_call(
        own_kernel,
        grid_spec=pltpu.PrefetchScalarGridSpec(
            num_scalar_prefetch=1, grid=(t,),
            in_specs=[pl.BlockSpec(memory_space=pltpu.SMEM)] + [spec] * 3, out_specs=[ospec, ospec]),
        out_shape=[jax.ShapeDtypeStruct((rows * n, cols), F32)] * 2,
        cost_estimate=cost(5, rows, cols), name="own", compiler_params=PARAMS,
    )(at, factor, w, m, g)


def squares_kernel(g_ref, o_ref, acc_ref):
    i = pl.program_id(0)
    rows, ff = g_ref.shape

    @pl.when(i == 0)
    def _():
        acc_ref[...] = jnp.zeros_like(acc_ref)

    for c in range(0, ff, LANES):
        g = g_ref[:, c:c + LANES]
        acc_ref[:, c:c + LANES] += jnp.sum((g * g).reshape(rows // 8, 8, LANES), axis=0)

    @pl.when(i == pl.num_programs(0) - 1)
    def _():
        parts = [acc_ref[:, c:c + LANES] for c in range(0, ff, LANES)]
        while len(parts) > 1:
            parts = [sum(parts[j:j + 2]) for j in range(0, len(parts), 2)]
        o_ref[...] = parts[0]


def squares(g):
    rows, ff = g.shape
    b = block_rows(rows, 0, 32)
    return pl.pallas_call(
        squares_kernel,
        grid=(rows // b,),
        in_specs=[pl.BlockSpec((b, ff), lambda i: (i, 0))],
        out_specs=pl.BlockSpec((8, LANES), lambda i: (0, 0)),
        out_shape=jax.ShapeDtypeStruct((8, LANES), F32),
        scratch_shapes=[pltpu.VMEM((8, ff), F32)],
        cost_estimate=cost(1, rows, ff), name="squares", compiler_params=PARAMS,
    )(g)


def parcels(k, n, rows):
    e = rows // 8
    if e % 8 == 0 and k == n - 1:
        return [(0, e), (e, 3 * e), (4 * e, 4 * e)]
    return [(0, rows)]


def plan(n):
    far = list(range(n - 1, 3, -1))
    near = [k for k in (3, 2, 1) if k < n]
    return far, near


def body(limit, n, nrow, grad, momentum, weight):
    me = lax.axis_index("col")
    rows, ff = weight.shape
    cols = ff // n
    far, near = plan(n)
    at = {k: jnp.reshape(me ^ k, (1,)).astype(jnp.int32) for k in range(n)}
    moved_w, moved_m = {}, {}

    def send_w(k):
        for j, (s, r) in enumerate(parcels(k, n, rows)):
            moved_w[k, j] = hop(cut(weight, at[k], cols, s, r), "col", k, n)

    for k in far + near:
        send_w(k)
    part = squares(grad)
    bits = rounds(n, nrow)
    for axis, k, size in bits:
        part = part + hop(part, axis, k, size)
    total = jnp.sum(part)
    factor = jnp.reshape(jnp.minimum(F32(1.0), limit / (jnp.sqrt(total) + F32(1e-06))), (1,))
    for k in far + near:
        for j, (s, r) in enumerate(parcels(k, n, rows)):
            moved_m[k, j] = hop(calc(momentum, grad, factor, at[k], cols, s, r), "col", k, n)
    outs = own(at[0], factor, weight, momentum, grad, n)
    for k in finish_order(n):
        for j, (s, r) in enumerate(parcels(k, n, rows)):
            outs = finish(at[k], moved_w[k, j], moved_m[k, j], outs, (rows * n, cols), rows, s)
    return tuple(outs)


def finish_order(n):
    first = [k for k in (1, 7, 6, 5, 3, 4, 2) if k < n]
    return list(range(n - 1, 7, -1)) + first


def rounds(n, nrow):
    col = [("col", 1 << j, n) for j in range(n.bit_length() - 1)]
    row = [("row", 1 << j, nrow) for j in range(nrow.bit_length() - 1)]
    return col[2:] + col[:1] + row + col[1:2]


def solution(mesh):
    spec = P(("row", "col"), None)
    n, nrow = mesh.shape["col"], mesh.shape["row"]

    def run(grad, momentum, weight):
        limit = F32(math.sqrt(grad.shape[0] * grad.shape[1]))
        f = jax.shard_map(lambda g, m, w: body(limit, n, nrow, g, m, w), mesh=mesh, in_specs=(spec,) * 3, out_specs=(P("row", "col"),) * 2, check_vma=False)
        return f(grad, momentum, weight)

    return run
```

time: 448 us -> 345 us (0.77)
  waiting for transfers between devices: 311 us -> 202 us
  Pallas kernels: 0 us -> 107 us
  local copies, waits for them, and re-layouts: 47 us -> 0 us
  blocking collectives: 42.2 us -> 0 us
  other arithmetic: 35 us -> 2.59 us
  starting transfers between devices: 11.1 us -> 30.4 us
    all_to_all x2 -> x0, waiting for transfers between devices: 311 us -> none  [the longest x1 161 us: body(): lax.all_to_all(local_weight, 'col', split_axis=1, concat_axis=0, tiled=True)]
    ppermute x0 -> x23, waiting for transfers between devices: none -> 202 us  [hop(): return lax.ppermute(x, axis, [(i, i ^ k) for i in range(n)])]
    pallas_call x0 -> x29, Pallas kernels: none -> 107 us  [the longest x9 34.3 us: finish(): pl.pallas_call(finish_kernel, grid_spec=pltpu.PrefetchScalarGridSpec(num_...]
    psum x1 -> x0, blocking collectives: 42.2 us -> none  [body(): total = lax.psum(jnp.sum(grad * grad), ('row', 'col'))]
    ppermute x0 -> x23, starting transfers between devices: none -> 30.4 us  [hop(): return lax.ppermute(x, axis, [(i, i ^ k) for i in range(n)])]
    sub x1 -> x0, other arithmetic: 25.5 us -> none  [update_state(): new_weight = weight - jnp.float32(0.1) * new_momentum]
    all_to_all x2 -> x0, local copies, waits for them, and re-layouts: 23.8 us -> none  [the longest x1 12 us: body(): lax.all_to_all(local_weight, 'col', split_axis=1, concat_axis=0, tiled=True)]
    unnamed x2 -> x0, local copies, waits for them, and re-layouts: 23.2 us -> none
  transfers between devices with their start and end apart: 2 -> 23, of which waited for: 2 -> 13; matrix products, arithmetic and copies ran while one was open for 3% -> 1% of each run, Pallas kernels for 0% -> 29%
where the time goes in v1:
time: 345 us; the launch traced here: 343 us
  waiting for transfers between devices  202 us (59%)
  Pallas kernels  107 us (31%)
  starting transfers between devices  30.4 us (9%)
    ppermute x23, waiting for transfers between devices, hop(): return lax.ppermute(x, axis, [(i, i ^ k) for i in range(n)])  202 us
    pallas_call x9, Pallas kernels, finish(): pl.pallas_call(finish_kernel, grid_spec=pltpu.PrefetchScalarGridSpec(num_...  34.3 us
    pallas_call x9, Pallas kernels, calc(): pl.pallas_call(calc_kernel, grid_spec=pltpu.PrefetchScalarGridSpec(num_sc...  31.4 us
    ppermute x23, starting transfers between devices, hop(): return lax.ppermute(x, axis, [(i, i ^ k) for i in range(n)])  30.4 us
    pallas_call x9, Pallas kernels, cut(): pl.pallas_call(copy_kernel, grid_spec=pltpu.PrefetchScalarGridSpec(num_sc...  28.6 us
    pallas_call x1, Pallas kernels, squares(): pl.pallas_call(squares_kernel, grid=(rows // b,), in_specs=[pl.BlockSpec(...  8.04 us
  transfers between devices with their start and end apart: 23, of which 13 were waited for; matrix products, arithmetic and copies ran while one was open for 1% of the time, Pallas kernels for 29%

profile of v1, /device:TPU:0, one launch (start us, length us, event | category | flops | bytes accessed | tf_op | source)
XLA Modules:
  0.0 343.2 jit_solution(10722862503144952891)
XLA Ops:
  0.6 3.7 %cut.17 = f32[256,1792]{1,0:T(8,128)} custom-call(s32[1]{0:T(128)} %bitcast.7.at, f32[256,14336]{1,0:T(8,128)} %w_ref.1), custom_call_target="tpu_custom_call" | custom-call | flops 1835008 | bytes 3670016 | tf_op jit(solution)/shard_map/cut/pallas_call | solution.py:40
  4.8 3.7 %cut.13 = f32[256,1792]{1,0:T(8,128)} custom-call(s32[1]{0:T(128)} %bitcast.5.at, f32[256,14336]{1,0:T(8,128)} %w_ref.1), custom_call_target="tpu_custom_call" | custom-call | flops 1835008 | bytes 3670016 | tf_op jit(solution)/shard_map/cut/pallas_call | solution.py:40
  14.9 8.0 %squares.1 = f32[8,128]{1,0:T(8,128)} custom-call(f32[256,14336]{1,0:T(8,128)} %g_ref.21), custom_call_target="tpu_custom_call" | custom-call | flops 14680064 | bytes 14680064 | tf_op jit(solution)/shard_map/squares/pallas_call | solution.py:141
  41.0 27.6 %collective-permute-done.5 = f32[8,128]{1,0:T(8,128)} collective-permute-done((f32[8,128]{1,0:T(8,128)}, f32[8,128]{1,0:T(8,128)}, u32[]{:S(2)}, u32[]{:S(2)}) %collective-permute-start.5) | collective-permute-done | bytes 4128 | tf_op jit(solution)/shard_map/ppermute | solution.py:16
  93.9 39.7 %collective-permute-done.18.m_ref = f32[96,1792]{1,0:T(8,128)} collective-permute-done((f32[96,1792]{1,0:T(8,128)}, f32[96,1792]{1,0:T(8,128)}, u32[]{:S(2)}, u32[]{:S(2)}) %collective-permute-start.18) | collective-permute-done | bytes 688160 | tf_op jit(solution)/shard_map/ppermute | solution.py:16
  136.0 4.1 %calc.17 = f32[256,1792]{1,0:T(8,128)} custom-call(s32[1]{0:T(128)} %bitcast.7.at, f32[1]{0:T(128)} %bitcast.1.factor, f32[256,14336]{1,0:T(8,128)} %m_ref.19, f32[256,14336]{1,0:T(8,128)} %g_ref.21), custom_call_target="tpu_custom_call" | custom-call | flops 1835008 | bytes 5505024 | tf_op jit(solution)/shard_map/calc/pallas_call | solution.py:59
  140.7 4.1 %calc.13 = f32[256,1792]{1,0:T(8,128)} custom-call(s32[1]{0:T(128)} %bitcast.5.at, f32[1]{0:T(128)} %bitcast.1.factor, f32[256,14336]{1,0:T(8,128)} %m_ref.19, f32[256,14336]{1,0:T(8,128)} %g_ref.21), custom_call_target="tpu_custom_call" | custom-call | flops 1835008 | bytes 5505024 | tf_op jit(solution)/shard_map/calc/pallas_call | solution.py:59
  144.8 4.0 %calc.12 = f32[256,1792]{1,0:T(8,128)} custom-call(s32[1]{0:T(128)} %bitcast.4.at, f32[1]{0:T(128)} %bitcast.1.factor, f32[256,14336]{1,0:T(8,128)} %m_ref.19, f32[256,14336]{1,0:T(8,128)} %g_ref.21), custom_call_target="tpu_custom_call" | custom-call | flops 1835008 | bytes 5505024 | tf_op jit(solution)/shard_map/calc/pallas_call | solution.py:59
  151.1 3.7 %cut.10 = f32[256,1792]{1,0:T(8,128)} custom-call(s32[1]{0:T(128)} %bitcast.2.at, f32[256,14336]{1,0:T(8,128)} %w_ref.1), custom_call_target="tpu_custom_call" | custom-call | flops 1835008 | bytes 3670016 | tf_op jit(solution)/shard_map/cut/pallas_call | solution.py:40
  158.6 4.1 %calc.11 = f32[256,1792]{1,0:T(8,128)} custom-call(s32[1]{0:T(128)} %bitcast.3.at, f32[1]{0:T(128)} %bitcast.1.factor, f32[256,14336]{1,0:T(8,128)} %m_ref.19, f32[256,14336]{1,0:T(8,128)} %g_ref.21), custom_call_target="tpu_custom_call" | custom-call | flops 1835008 | bytes 5505024 | tf_op jit(solution)/shard_map/calc/pallas_call | solution.py:59
  162.6 14.1 %collective-permute-done.11.w_ref = f32[256,1792]{1,0:T(8,128)} collective-permute-done((f32[256,1792]{1,0:T(8,128)}, f32[256,1792]{1,0:T(8,128)}, u32[]{:S(2)}, u32[]{:S(2)}) %collective-permute-start.11) | collective-permute-done | bytes 1835040 | tf_op jit(solution)/shard_map/ppermute | solution.py:16
  178.8 4.0 %calc.10 = f32[256,1792]{1,0:T(8,128)} custom-call(s32[1]{0:T(128)} %bitcast.2.at, f32[1]{0:T(128)} %bitcast.1.factor, f32[256,14336]{1,0:T(8,128)} %m_ref.19, f32[256,14336]{1,0:T(8,128)} %g_ref.21), custom_call_target="tpu_custom_call" | custom-call | flops 1835008 | bytes 5505024 | tf_op jit(solution)/shard_map/calc/pallas_call | solution.py:59
  184.9 4.1 %calc.9 = f32[256,1792]{1,0:T(8,128)} custom-call(s32[1]{0:T(128)} %bitcast.at, f32[1]{0:T(128)} %bitcast.1.factor, f32[256,14336]{1,0:T(8,128)} %m_ref.19, f32[256,14336]{1,0:T(8,128)} %g_ref.21), custom_call_target="tpu_custom_call" | custom-call | flops 1835008 | bytes 5505024 | tf_op jit(solution)/shard_map/calc/pallas_call | solution.py:59
  188.9 33.2 %collective-permute-done.14.m_ref = f32[256,1792]{1,0:T(8,128)} collective-permute-done((f32[256,1792]{1,0:T(8,128)}, f32[256,1792]{1,0:T(8,128)}, u32[]{:S(2)}, u32[]{:S(2)}) %collective-permute-start.14) | collective-permute-done | bytes 1835040 | tf_op jit(solution)/shard_map/ppermute | solution.py:16
  224.0 31.4 %collective-permute-done.12.m_ref = f32[256,1792]{1,0:T(8,128)} collective-permute-done((f32[256,1792]{1,0:T(8,128)}, f32[256,1792]{1,0:T(8,128)}, u32[]{:S(2)}, u32[]{:S(2)}) %collective-permute-start.12) | collective-permute-done | bytes 1835040 | tf_op jit(solution)/shard_map/ppermute | solution.py:16
  257.1 4.9 %own.1 = (f32[2048,1792]{1,0:T(8,128)}, f32[2048,1792]{1,0:T(8,128)}) custom-call(s32[1]{0:T(128)} %bitcast.8.at, f32[1]{0:T(128)} %bitcast.1.factor, f32[256,14336]{1,0:T(8,128)} %w_ref.1, f32[256,14336]{1,0:T(8,128)} %m_ref.19, f32[256,14336]{1,0:T(8,128)} %g_ref.21), custom_call_target="tpu_custom_call" | custom-call | flops 1835008 | bytes 9175040 | tf_op jit(solution)/shard_map/own/pallas_call | solution.py:108
  262.0 4.5 %finish.9 = (f32[2048,1792]{1,0:T(8,128)}, f32[2048,1792]{1,0:T(8,128)}) custom-call(s32[1]{0:T(128)} %bitcast.7.at, f32[256,1792]{1,0:T(8,128)} %collective-permute-done.21.w_ref, f32[256,1792]{1,0:T(8,128)} %collective-permute-done.22.m_ref, f32[2048,1792]{1,0:T(8,128)} %get-tuple-element.20.refs_0_, ...), custom_call_target="tpu_custom_call", output_to_operand_aliasing={{0}: (3, {}), {1}: (4, {})} | custom-call | flops 1835008 | bytes 7340032 | tf_op jit(solution)/shard_map/finish/pallas_call | solution.py:85
  274.1 4.5 %finish.13 = (f32[2048,1792]{1,0:T(8,128)}, f32[2048,1792]{1,0:T(8,128)}) custom-call(s32[1]{0:T(128)} %bitcast.5.at, f32[256,1792]{1,0:T(8,128)} %collective-permute-done.13.w_ref, f32[256,1792]{1,0:T(8,128)} %collective-permute-done.14.m_ref, f32[2048,1792]{1,0:T(8,128)} %get-tuple-element.28.refs_0_, ...), custom_call_target="tpu_custom_call", output_to_operand_aliasing={{0}: (3, {}), {1}: (4, {})} | custom-call | flops 1835008 | bytes 7340032 | tf_op jit(solution)/shard_map/finish/pallas_call | solution.py:85
  278.5 4.5 %finish.14 = (f32[2048,1792]{1,0:T(8,128)}, f32[2048,1792]{1,0:T(8,128)}) custom-call(s32[1]{0:T(128)} %bitcast.4.at, f32[256,1792]{1,0:T(8,128)} %collective-permute-done.11.w_ref, f32[256,1792]{1,0:T(8,128)} %collective-permute-done.12.m_ref, f32[2048,1792]{1,0:T(8,128)} %get-tuple-element.30.refs_0_, ...), custom_call_target="tpu_custom_call", output_to_operand_aliasing={{0}: (3, {}), {1}: (4, {})} | custom-call | flops 1835008 | bytes 7340032 | tf_op jit(solution)/shard_map/finish/pallas_call | solution.py:85
  283.0 4.5 %finish.15 = (f32[2048,1792]{1,0:T(8,128)}, f32[2048,1792]{1,0:T(8,128)}) custom-call(s32[1]{0:T(128)} %bitcast.3.at, f32[256,1792]{1,0:T(8,128)} %collective-permute-done.9.w_ref, f32[256,1792]{1,0:T(8,128)} %collective-permute-done.10.m_ref, f32[2048,1792]{1,0:T(8,128)} %get-tuple-element.32.refs_0_, ...), custom_call_target="tpu_custom_call", output_to_operand_aliasing={{0}: (3, {}), {1}: (4, {})} | custom-call | flops 1835008 | bytes 7340032 | tf_op jit(solution)/shard_map/finish/pallas_call | solution.py:85
  287.5 8.2 %collective-permute-done.7.w_ref = f32[256,1792]{1,0:T(8,128)} collective-permute-done((f32[256,1792]{1,0:T(8,128)}, f32[256,1792]{1,0:T(8,128)}, u32[]{:S(2)}, u32[]{:S(2)}) %collective-permute-start.7) | collective-permute-done | bytes 1835040 | tf_op jit(solution)/shard_map/ppermute | solution.py:16
  295.7 38.5 %collective-permute-done.8.m_ref = f32[256,1792]{1,0:T(8,128)} collective-permute-done((f32[256,1792]{1,0:T(8,128)}, f32[256,1792]{1,0:T(8,128)}, u32[]{:S(2)}, u32[]{:S(2)}) %collective-permute-start.8) | collective-permute-done | bytes 1835040 | tf_op jit(solution)/shard_map/ppermute | solution.py:16
  334.2 4.4 %finish.16 = (f32[2048,1792]{1,0:T(8,128)}, f32[2048,1792]{1,0:T(8,128)}) custom-call(s32[1]{0:T(128)} %bitcast.2.at, f32[256,1792]{1,0:T(8,128)} %collective-permute-done.7.w_ref, f32[256,1792]{1,0:T(8,128)} %collective-permute-done.8.m_ref, f32[2048,1792]{1,0:T(8,128)} %get-tuple-element.34.refs_0_, ...), custom_call_target="tpu_custom_call", output_to_operand_aliasing={{0}: (3, {}), {1}: (4, {})} | custom-call | flops 1835008 | bytes 7340032 | tf_op jit(solution)/shard_map/finish/pallas_call | solution.py:85
  338.8 4.4 %finish.17 = (f32[2048,1792]{1,0:T(8,128)}, f32[2048,1792]{1,0:T(8,128)}) custom-call(s32[1]{0:T(128)} %bitcast.at, f32[256,1792]{1,0:T(8,128)} %collective-permute-done.w_ref, f32[256,1792]{1,0:T(8,128)} %collective-permute-done.6.m_ref, f32[2048,1792]{1,0:T(8,128)} %get-tuple-element.36.refs_0_, ...), custom_call_target="tpu_custom_call", output_to_operand_aliasing={{0}: (3, {}), {1}: (4, {})} | custom-call | flops 1835008 | bytes 7340032 | tf_op jit(solution)/shard_map/finish/pallas_call | solution.py:85
  (56 shorter events, 74.0 us)
Async XLA Ops:
  4.4 144.4 %collective-permute-start.21 = (f32[256,1792]{1,0:T(8,128)}, f32[256,1792]{1,0:T(8,128)}, u32[]{:S(2)}, u32[]{:S(2)}) collective-permute-start(f32[256,1792]{1,0:T(8,128)} %cut.17), channel_id=1, source_target_pairs={{0,1},{1,0},{2,3},{3,2},{4,5},{5,4},{6,7},{7,6},{8,9},{9,8},{10,11... | collective-permute-start | bytes 5505032 | tf_op jit(solution)/shard_map/ppermute | solution.py:16
  8.6 141.7 %collective-permute-start.13 = (f32[256,1792]{1,0:T(8,128)}, f32[256,1792]{1,0:T(8,128)}, u32[]{:S(2)}, u32[]{:S(2)}) collective-permute-start(f32[256,1792]{1,0:T(8,128)} %cut.13), channel_id=1, source_target_pairs={{0,6},{1,7},{2,4},{3,5},{4,2},{5,3},{6,0},{7,1},{8,14},{9,15},{10,... | collective-permute-start | bytes 5505032 | tf_op jit(solution)/shard_map/ppermute | solution.py:16
  14.8 69.7 %collective-permute-start.17 = (f32[96,1792]{1,0:T(8,128)}, f32[96,1792]{1,0:T(8,128)}, u32[]{:S(2)}, u32[]{:S(2)}) collective-permute-start(f32[96,1792]{1,0:T(8,128)} %cut.15), channel_id=1, source_target_pairs={{0,7},{1,6},{2,5},{3,4},{4,3},{5,2},{6,1},{7,0},{8,15},{9,14},{10,... | collective-permute-start | bytes 2064392 | tf_op jit(solution)/shard_map/ppermute | solution.py:16
  22.9 4.2 %collective-permute-start.1 = (f32[8,128]{1,0:T(8,128)}, f32[8,128]{1,0:T(8,128)S(1)}, u32[]{:S(2)}, u32[]{:S(2)}) collective-permute-start(f32[8,128]{1,0:T(8,128)} %squares.1), channel_id=1, source_target_pairs={{0,4},{1,5},{2,6},{3,7},{4,0},{5,1},{6,2},{7,3},{8,12},{9,13},{10,... | collective-permute-start | bytes 12296 | tf_op jit(solution)/shard_map/ppermute | solution.py:16
  27.8 1.2 collective-permute-start.2
  29.0 3.6 %collective-permute-start.3 = (f32[8,128]{1,0:T(8,128)S(1)}, f32[8,128]{1,0:T(8,128)S(1)}, u32[]{:S(2)}, u32[]{:S(2)}) collective-permute-start(f32[8,128]{1,0:T(8,128)S(1)} %add.19), channel_id=1, source_target_pairs={{0,8},{8,0},{16,24},{24,16},{1,9},{9,1},{17,25},{25,17},{2,10},{10... | collective-permute-start | bytes 12296 | tf_op jit(solution)/shard_map/ppermute | solution.py:16
  32.6 4.5 %collective-permute-start.4 = (f32[8,128]{1,0:T(8,128)S(1)}, f32[8,128]{1,0:T(8,128)S(1)}, u32[]{:S(2)}, u32[]{:S(2)}) collective-permute-start(f32[8,128]{1,0:T(8,128)S(1)} %add.20), channel_id=1, source_target_pairs={{0,16},{8,24},{16,0},{24,8},{1,17},{9,25},{17,1},{25,9},{2,18},{10... | collective-permute-start | bytes 12296 | tf_op jit(solution)/shard_map/ppermute | solution.py:16
  37.7 30.9 %collective-permute-start.5 = (f32[8,128]{1,0:T(8,128)}, f32[8,128]{1,0:T(8,128)}, u32[]{:S(2)}, u32[]{:S(2)}) collective-permute-start(f32[8,128]{1,0:T(8,128)} %add.21), channel_id=1, source_target_pairs={{0,2},{1,3},{2,0},{3,1},{4,6},{5,7},{6,4},{7,5},{8,10},{9,11},{10,... | collective-permute-start | bytes 12296 | tf_op jit(solution)/shard_map/ppermute | solution.py:16
  41.0 35.8 %collective-permute-start.19 = (f32[32,1792]{1,0:T(8,128)}, f32[32,1792]{1,0:T(8,128)}, u32[]{:S(2)}, u32[]{:S(2)}) collective-permute-start(f32[32,1792]{1,0:T(8,128)} %cut.16), channel_id=1, source_target_pairs={{0,7},{1,6},{2,5},{3,4},{4,3},{5,2},{6,1},{7,0},{8,15},{9,14},{10,... | collective-permute-start | bytes 688136 | tf_op jit(solution)/shard_map/ppermute | solution.py:16
  72.4 8.4 %collective-permute-start.20 = (f32[32,1792]{1,0:T(8,128)}, f32[32,1792]{1,0:T(8,128)}, u32[]{:S(2)}, u32[]{:S(2)}) collective-permute-start(f32[32,1792]{1,0:T(8,128)} %calc.16), channel_id=1, source_target_pairs={{0,7},{1,6},{2,5},{3,4},{4,3},{5,2},{6,1},{7,0},{8,15},{9,14},{10,... | collective-permute-start | bytes 688136 | tf_op jit(solution)/shard_map/ppermute | solution.py:16
  76.8 63.3 %collective-permute-start.15 = (f32[128,1792]{1,0:T(8,128)}, f32[128,1792]{1,0:T(8,128)}, u32[]{:S(2)}, u32[]{:S(2)}) collective-permute-start(f32[128,1792]{1,0:T(8,128)} %cut.14), channel_id=1, source_target_pairs={{0,7},{1,6},{2,5},{3,4},{4,3},{5,2},{6,1},{7,0},{8,15},{9,14},{10,... | collective-permute-start | bytes 2752520 | tf_op jit(solution)/shard_map/ppermute | solution.py:16
  80.8 59.3 %collective-permute-start.16 = (f32[128,1792]{1,0:T(8,128)}, f32[128,1792]{1,0:T(8,128)}, u32[]{:S(2)}, u32[]{:S(2)}) collective-permute-start(f32[128,1792]{1,0:T(8,128)} %calc.14), channel_id=1, source_target_pairs={{0,7},{1,6},{2,5},{3,4},{4,3},{5,2},{6,1},{7,0},{8,15},{9,14},{10,... | collective-permute-start | bytes 2752520 | tf_op jit(solution)/shard_map/ppermute | solution.py:16
  84.5 49.1 %collective-permute-start.18 = (f32[96,1792]{1,0:T(8,128)}, f32[96,1792]{1,0:T(8,128)}, u32[]{:S(2)}, u32[]{:S(2)}) collective-permute-start(f32[96,1792]{1,0:T(8,128)} %calc.15), channel_id=1, source_target_pairs={{0,7},{1,6},{2,5},{3,4},{4,3},{5,2},{6,1},{7,0},{8,15},{9,14},{10,... | collective-permute-start | bytes 2064392 | tf_op jit(solution)/shard_map/ppermute | solution.py:16
  133.6 43.2 %collective-permute-start.11 = (f32[256,1792]{1,0:T(8,128)}, f32[256,1792]{1,0:T(8,128)}, u32[]{:S(2)}, u32[]{:S(2)}) collective-permute-start(f32[256,1792]{1,0:T(8,128)} %cut.12), channel_id=1, source_target_pairs={{0,5},{1,4},{2,7},{3,6},{4,1},{5,0},{6,3},{7,2},{8,13},{9,12},{10,... | collective-permute-start | bytes 5505032 | tf_op jit(solution)/shard_map/ppermute | solution.py:16
  140.1 42.7 %collective-permute-start.9 = (f32[256,1792]{1,0:T(8,128)}, f32[256,1792]{1,0:T(8,128)}, u32[]{:S(2)}, u32[]{:S(2)}) collective-permute-start(f32[256,1792]{1,0:T(8,128)} %cut.11), channel_id=1, source_target_pairs={{0,3},{1,2},{2,1},{3,0},{4,7},{5,6},{6,5},{7,4},{8,11},{9,10},{10,... | collective-permute-start | bytes 5505032 | tf_op jit(solution)/shard_map/ppermute | solution.py:16
  140.1 43.4 %collective-permute-start.22 = (f32[256,1792]{1,0:T(8,128)}, f32[256,1792]{1,0:T(8,128)}, u32[]{:S(2)}, u32[]{:S(2)}) collective-permute-start(f32[256,1792]{1,0:T(8,128)} %calc.17), channel_id=1, source_target_pairs={{0,1},{1,0},{2,3},{3,2},{4,5},{5,4},{6,7},{7,6},{8,9},{9,8},{10,11... | collective-permute-start | bytes 5505032 | tf_op jit(solution)/shard_map/ppermute | solution.py:16
  148.8 73.3 %collective-permute-start.14 = (f32[256,1792]{1,0:T(8,128)}, f32[256,1792]{1,0:T(8,128)}, u32[]{:S(2)}, u32[]{:S(2)}) collective-permute-start(f32[256,1792]{1,0:T(8,128)} %calc.13), channel_id=1, source_target_pairs={{0,6},{1,7},{2,4},{3,5},{4,2},{5,3},{6,0},{7,1},{8,14},{9,15},{10,... | collective-permute-start | bytes 5505032 | tf_op jit(solution)/shard_map/ppermute | solution.py:16
  150.3 105.1 %collective-permute-start.12 = (f32[256,1792]{1,0:T(8,128)}, f32[256,1792]{1,0:T(8,128)}, u32[]{:S(2)}, u32[]{:S(2)}) collective-permute-start(f32[256,1792]{1,0:T(8,128)} %calc.12), channel_id=1, source_target_pairs={{0,5},{1,4},{2,7},{3,6},{4,1},{5,0},{6,3},{7,2},{8,13},{9,12},{10,... | collective-permute-start | bytes 5505032 | tf_op jit(solution)/shard_map/ppermute | solution.py:16
  176.8 106.3 %collective-permute-start.10 = (f32[256,1792]{1,0:T(8,128)}, f32[256,1792]{1,0:T(8,128)}, u32[]{:S(2)}, u32[]{:S(2)}) collective-permute-start(f32[256,1792]{1,0:T(8,128)} %calc.11), channel_id=1, source_target_pairs={{0,3},{1,2},{2,1},{3,0},{4,7},{5,6},{6,5},{7,4},{8,11},{9,10},{10,... | collective-permute-start | bytes 5505032 | tf_op jit(solution)/shard_map/ppermute | solution.py:16
  182.8 112.8 %collective-permute-start.7 = (f32[256,1792]{1,0:T(8,128)}, f32[256,1792]{1,0:T(8,128)}, u32[]{:S(2)}, u32[]{:S(2)}) collective-permute-start(f32[256,1792]{1,0:T(8,128)} %cut.10), channel_id=1, source_target_pairs={{0,4},{1,5},{2,6},{3,7},{4,0},{5,1},{6,2},{7,3},{8,12},{9,13},{10,... | collective-permute-start | bytes 5505032 | tf_op jit(solution)/shard_map/ppermute | solution.py:16
  183.5 150.7 %collective-permute-start.8 = (f32[256,1792]{1,0:T(8,128)}, f32[256,1792]{1,0:T(8,128)}, u32[]{:S(2)}, u32[]{:S(2)}) collective-permute-start(f32[256,1792]{1,0:T(8,128)} %calc.10), channel_id=1, source_target_pairs={{0,4},{1,5},{2,6},{3,7},{4,0},{5,1},{6,2},{7,3},{8,12},{9,13},{10,... | collective-permute-start | bytes 5505032 | tf_op jit(solution)/shard_map/ppermute | solution.py:16
  222.1 116.6 %collective-permute-start = (f32[256,1792]{1,0:T(8,128)}, f32[256,1792]{1,0:T(8,128)}, u32[]{:S(2)}, u32[]{:S(2)}) collective-permute-start(f32[256,1792]{1,0:T(8,128)} %cut.9), channel_id=1, source_target_pairs={{0,2},{1,3},{2,0},{3,1},{4,6},{5,7},{6,4},{7,5},{8,10},{9,11},{10,... | collective-permute-start | bytes 5505032 | tf_op jit(solution)/shard_map/ppermute | solution.py:16
  255.4 83.4 %collective-permute-start.6 = (f32[256,1792]{1,0:T(8,128)}, f32[256,1792]{1,0:T(8,128)}, u32[]{:S(2)}, u32[]{:S(2)}) collective-permute-start(f32[256,1792]{1,0:T(8,128)} %calc.9), channel_id=1, source_target_pairs={{0,2},{1,3},{2,0},{3,1},{4,6},{5,7},{6,4},{7,5},{8,10},{9,11},{10,... | collective-permute-start | bytes 5505032 | tf_op jit(solution)/shard_map/ppermute | solution.py:16
